TPU v7x, 256 devices: a whole 4x4x8 slice. The times are simulated.
256 devices in a mesh: macro: 128 (over y, x_lo, z, core), micro: 2 (over x_hi).
Axes of the slice: x: 4 (x_hi: 2, x_lo: 2; x = x_hi * 2 + x_lo), y: 4, z: 8, core: 2. Of those that a mesh axis runs over, the one named last changes fastest.
Arguments:
- macro_state: float32 [65536, 128], P('macro'), may hold values from -6 to 6
- micro_state: bfloat16 [65536, 12, 512], P('macro', None, 'micro'), may hold values from -6 to 6
- velocity: float32 [65536], P('macro'), may hold values from 0.25 to 4
- propagator: bfloat16 [512, 512], P(None, 'micro'), may hold values from -1 to 1
- forcing_map: float32 [128, 512], P(None, 'micro'), may hold values from -0.5 to 0.5
- readout: float32 [128, 512], P(None, 'micro'), may hold values from -1 to 1
- speed_weights: float32 [128], replicated, may hold values from -0.5 to 0.5
Outputs:
- macro_next: float32 [65536, 128], P('macro')
- micro_final: bfloat16 [65536, 12, 512], P('macro', None, 'micro')
All inputs are finite; a program needn't handle non-finite values.
Results may differ from a plain program's by a relative error of at most 0.006.
Values may be sent and summed in bfloat16 or wider, within the bound.
No kernel may reach another device: no remote copies, remote signals or barrier semaphores. Data moves between devices by JAX's collectives and lax.ppermute only.
A program may use at most 64 MiB of HBM per device.

v0:
```python
import jax
import jax.numpy as jnp
from jax import lax
from jax.sharding import Mesh
from jax.sharding import PartitionSpec as P

S = 12
STEPS = 4
MACRO = ("macro_0", "macro_1", "macro_2", "macro_3")


def laid_out(blocks, dim):
    blocks = jnp.moveaxis(blocks, 0, dim)
    dims = blocks.shape
    return blocks.reshape(*dims[:dim], dims[dim] * dims[dim + 1], *dims[dim + 2 :])


def sent_to_all(array, axis):
    copies = jnp.broadcast_to(array, (lax.axis_size(axis), *array.shape))
    return lax.all_to_all(copies, axis, split_axis=0, concat_axis=0, tiled=True)


def gathered_copies(array, axis, dim):
    return laid_out(sent_to_all(array, axis), dim)


def side_by_side(arrays, axis, dim, along):
    widths = [a.shape[along] for a in arrays]
    both = jnp.concatenate(arrays, axis=along)
    result = gathered_copies(both, axis, dim)
    return tuple(jnp.split(result, [sum(widths[:k]) for k in range(1, len(widths))], axis=along))


def taken_together(array, axis):
    everything = sent_to_all(array, axis)
    return jnp.sum(everything.astype(jnp.float32), axis=0)


def cut_along(array, dim, size):
    before, after = (array.shape[:dim], array.shape[dim + 1 :])
    return jnp.moveaxis(array.reshape(*before, size, -1, *after), dim, 0)


def piece_ends(length, count):
    unit = 8 if length >= 8 * count else 1
    return [length // unit * k // count * unit for k in range(1, count)]


def cut_exchange(array, axis, pieces, split_dim, concat_dim):
    blocks = cut_along(array, split_dim, lax.axis_size(axis))
    split_at = max(range(1, max(2, blocks.ndim - 1)), key=lambda d: blocks.shape[d])
    outs = []
    for section in jnp.split(blocks, piece_ends(blocks.shape[split_at], pieces), axis=split_at):
        if section.size:
            outs.append(lax.all_to_all(section, axis, split_axis=0, concat_axis=0, tiled=True))
    return laid_out(jnp.concatenate(outs, axis=split_at), concat_dim)


def by_axis(array, axes):
    for axis in axes:
        array = lax.pmax(array, axis)
    return array


def from_behind(value, axis, steps):
    count = lax.axis_size(axis)
    pairs = [(source, (source + steps) % count) for source in range(count)]
    return lax.ppermute(value, axis, pairs)


def shards(macro_state, micro_state, velocity, propagator, forcing_map, readout, speed_weights):
    highest = lax.Precision.HIGHEST
    coupling = gathered_copies(propagator, "micro", 1)
    forcing_full, readout_full = side_by_side((forcing_map, readout), "micro", 1, 0)
    forcing = jnp.tanh(
        jnp.dot(macro_state, forcing_full, precision=highest, preferred_element_type=jnp.float32)
    )
    micro_now = lax.all_to_all(micro_state, "micro", split_axis=1, concat_axis=2, tiled=True)
    tanh_sum = jnp.zeros(forcing.shape, jnp.float32)
    width = micro_now.shape[2]
    for _ in range(STEPS):
        summed = jnp.dot(micro_now.reshape(-1, width), coupling, preferred_element_type=jnp.float32)
        summed = summed.reshape(micro_now.shape)
        micro_now = (summed + forcing[:, None, :]).astype(jnp.bfloat16)
        tanh_sum = tanh_sum + jnp.sum(jnp.tanh(micro_now.astype(jnp.float32)), axis=1)
    partial_value = jnp.dot(
        tanh_sum / (STEPS * S),
        readout_full.T,
        precision=highest,
        preferred_element_type=jnp.float32,
    )
    forces = taken_together(partial_value.astype(jnp.bfloat16), "micro").astype(jnp.float32)
    micro_final = cut_exchange(micro_now, "micro", 2, 2, 1)
    drive_in = jnp.dot(forces, speed_weights, precision=highest, preferred_element_type=jnp.float32)
    speeds = velocity * (1.5 + jnp.tanh(drive_in))
    fastest = by_axis(jnp.max(speeds), MACRO)
    time_step = 0.8 / jnp.maximum(fastest, 1.0)
    fluxes = speeds[:, None] * macro_state
    stacked = jnp.stack([macro_state, fluxes])
    ahead_rows = from_behind(stacked[:, :1], MACRO, -1)
    state_after = jnp.concatenate([macro_state[1:], ahead_rows[0]], axis=0)
    flux_after = jnp.concatenate([fluxes[1:], ahead_rows[1]], axis=0)
    interface = 0.5 * (fluxes + flux_after) - 0.5 * fastest * (state_after - macro_state)
    carried = from_behind(interface[-1:], MACRO, 1)
    interface_before = jnp.concatenate([carried, interface[:-1]], axis=0)
    macro_next = macro_state - time_step * (interface - interface_before) + time_step * forces
    return (macro_next, micro_final)


def solution(mesh):
    torus = Mesh(
        mesh.devices.reshape(4, 2, 8, 2, mesh.shape["micro"]),
        ("macro_0", "macro_1", "macro_2", "macro_3", "micro"),
    )
    placed = (
        P(MACRO, None),
        P(MACRO, None, "micro"),
        P(MACRO),
        P(None, "micro"),
        P(None, "micro"),
        P(None, "micro"),
        P(),
    )
    return jax.shard_map(
        shards,
        mesh=torus,
        in_specs=placed,
        out_specs=(P(MACRO, None), P(MACRO, None, "micro")),
        check_vma=False,
    )
```

profile of v0, /device:TPU:4, one launch (start us, length us, event | category | flops | bytes accessed | tf_op | source)
XLA Modules:
  0.0 182.2 jit_solution(6250397391435274117)
XLA Ops:
  1.8 10.9 %all_to_all.40 = f32[2,256,256]{1,2,0:T(8,128)} all-to-all(f32[2,256,256]{1,2,0:T(8,128)S(1)} %broadcast_in_dim.7), channel_id=1, replica_groups=mesh['macro_0'=4,'macro_1'=2,'macro_2'=8,'macro_3'=2,'micro'=2] {'micro'}, dimensions={0} | all-to-all | bytes 1048576 | tf_op jit(solution)/shard_map/all_to_all | solution.py:20
  13.7 11.1 %all_to_all.41 = bf16[2,512,256]{2,1,0:T(8,128)(2,1)} all-to-all(bf16[2,512,256]{2,1,0:T(8,128)(2,1)S(1)} %broadcast_in_dim.6), channel_id=1, replica_groups=mesh['macro_0'=4,'macro_1'=2,'macro_2'=8,'macro_3'=2,'micro'=2] {'micro'}, dimensions={0} | all-to-all | bytes 1048576 | tf_op jit(solution)/shard_map/all_to_all | solution.py:20
  24.9 7.3 %all-to-all-start = ((bf16[512,12,256]{2,0,1:T(8,128)(2,1)}), bf16[512,12,256]{2,0,1:T(8,128)(2,1)S(1)}, u32[]{:S(2)}, u32[]{:S(2)}) async-start(bf16[512,12,256]{2,0,1:T(8,128)(2,1)} %param.8), calls=%async_computation | async-start | bytes 6291456 | tf_op jit(solution)/shard_map/all_to_all | solution.py:78
  32.1 2.4 %copy.28 = bf16[512,2,256]{2,1,0:T(2,128)(2,1)} copy(bf16[512,2,256]{2,0,1:T(8,128)(2,1)} %bitcast.53) | data formatting | bytes 1048576 | tf_op jit(solution)/shard_map/transpose | solution.py:13
  34.6 2.1 %copy.36 = bf16[512,2,256]{0,2,1:T(8,128)(2,1)} copy(bf16[512,2,256]{2,0,1:T(8,128)(2,1)} %bitcast.54) | data formatting | bytes 1048576 | tf_op jit(solution)/shard_map/reshape | solution.py:15
  40.4 2.5 %copy.30 = f32[512,512]{1,0:T(8,128)} copy(f32[512,512]{0,1:T(8,128)} %fusion) | data formatting | bytes 2097152 | tf_op jit(solution)/shard_map/tanh | solution.py:75
  42.9 2.2 %reshape.38 = bf16[512,512,1]{1,0,2:T(8,128)(2,1)} reshape(bf16[512,2,256]{2,1,0:T(2,128)(2,1)} %copy.28) | data formatting | bytes 1048576 | tf_op jit(solution)/shard_map/reshape | solution.py:15
  45.1 18.7 %all-to-all-done = bf16[512,12,256]{2,0,1:T(8,128)(2,1)S(1)} async-done(((bf16[512,12,256]{2,0,1:T(8,128)(2,1)}), bf16[512,12,256]{2,0,1:T(8,128)(2,1)S(1)}, u32[]{:S(2)}, u32[]{:S(2)}) %all-to-all-start) | async-done | bytes 3145760 | tf_op jit(solution)/shard_map/all_to_all | solution.py:78
  63.8 4.9 %copy.42 = bf16[512,2,6,256]{3,1,0,2:T(2,128)(2,1)} copy(bf16[512,2,6,256]{3,0,2,1:T(8,128)(2,1)S(1)} %bitcast.49) | data formatting | bytes 6291456 | tf_op jit(solution)/shard_map/all_to_all | solution.py:78
  68.7 4.6 %dot_general.23 = bf16[512,6,512]{2,0,1:T(8,128)(2,1)S(1)} reshape(bf16[512,6,2,256]{3,2,0,1:T(2,128)(2,1)} %bitcast.51) | data formatting | bytes 6291456 | tf_op jit(solution)/shard_map/dot_general | solution.py:82
  73.3 3.8 %tanh_reduce_fusion.3 = (f32[512,512]{1,0:T(8,128)S(1)}, bf16[512,6,512]{2,0,1:T(8,128)(2,1)S(1)}) fusion(f32[512,512]{1,0:T(8,128)} %copy.30, bf16[512,6,512]{2,0,1:T(8,128)(2,1)S(1)} %dot_general.23, bf16[512,512,1]{1,0,2:T(8,128)(2,1)} %reshape.38), kind=kOutput, calls=%fused_computation.6 | convolution fusion | flops 1616642048 | bytes 8912896 | tf_op jit(solution)/shard_map/dot_general | solution.py:82
  77.1 2.1 %tanh_reduce_fusion.2 = (f32[512,512]{1,0:T(8,128)S(1)}, bf16[512,6,512]{2,0,1:T(8,128)(2,1)S(1)}) fusion(f32[512,512]{1,0:T(8,128)S(1)} %copy-done.4, bf16[512,6,512]{2,0,1:T(8,128)(2,1)S(1)} %get-tuple-element.17, bf16[512,512,1]{1,0,2:T(8,128)(2,1)S(1)} %copy-done.7), kind=kOutput, calls=%fused_computation.4 | convolution fusion | flops 1616642048 | bytes 8912896 | tf_op jit(solution)/shard_map/dot_general | solution.py:82
  79.2 2.1 %tanh_reduce_fusion.1 = (f32[512,512]{1,0:T(8,128)S(1)}, bf16[512,6,512]{2,0,1:T(8,128)(2,1)S(1)}) fusion(f32[512,512]{1,0:T(8,128)S(1)} %copy-done.4, bf16[512,6,512]{2,0,1:T(8,128)(2,1)S(1)} %get-tuple-element.19, bf16[512,512,1]{1,0,2:T(8,128)(2,1)S(1)} %copy-done.7), kind=kOutput, calls=%fused_computation.2 | convolution fusion | flops 1616642048 | bytes 8912896 | tf_op jit(solution)/shard_map/dot_general | solution.py:82
  81.3 2.1 %tanh_reduce_fusion = (f32[512,512]{1,0:T(8,128)S(1)}, bf16[512,6,512]{2,0,1:T(8,128)(2,1)S(1)}) fusion(f32[512,512]{1,0:T(8,128)S(1)} %copy-done.4, bf16[512,6,512]{2,0,1:T(8,128)(2,1)S(1)} %get-tuple-element.15, bf16[512,512,1]{0,1,2:T(8,128)(2,1)S(1)} %bitcast.61), kind=kOutput, calls=%fused_computation | convolution fusion | flops 1616642048 | bytes 8912896 | tf_op jit(solution)/shard_map/dot_general | solution.py:82
  85.2 7.3 %all-to-all-start.3 = ((bf16[2,512,128]{2,1,0:T(8,128)(2,1)}), bf16[2,512,128]{2,1,0:T(8,128)(2,1)}, u32[]{:S(2)}, u32[]{:S(2)}) async-start(bf16[2,512,128]{2,1,0:T(8,128)(2,1)} %broadcast_in_dim.16), calls=%async_computation.3 | async-start | bytes 524288 | tf_op jit(solution)/shard_map/all_to_all | solution.py:20
  95.8 7.2 %all-to-all-start.5 = ((bf16[2,256,6,256]{3,1,2,0:T(8,128)(2,1)}), bf16[2,256,6,256]{3,1,2,0:T(8,128)(2,1)S(1)}, u32[]{:S(2)}, u32[]{:S(2)}) async-start(bf16[2,256,6,256]{3,1,2,0:T(8,128)(2,1)} %get-tuple-element.5), calls=%async_computation.5 | async-start | bytes 3145728 | tf_op jit(solution)/shard_map/all_to_all | solution.py:55
  106.6 9.2 %all-to-all-done.5 = bf16[2,256,6,256]{3,1,2,0:T(8,128)(2,1)S(1)} async-done(((bf16[2,256,6,256]{3,1,2,0:T(8,128)(2,1)}), bf16[2,256,6,256]{3,1,2,0:T(8,128)(2,1)S(1)}, u32[]{:S(2)}, u32[]{:S(2)}) %all-to-all-start.5) | async-done | bytes 1572896 | tf_op jit(solution)/shard_map/all_to_all | solution.py:55
  115.8 6.9 %all-to-all-start.4 = ((bf16[2,256,6,256]{3,1,2,0:T(8,128)(2,1)}), bf16[2,256,6,256]{3,1,2,0:T(8,128)(2,1)S(1)}, u32[]{:S(2)}, u32[]{:S(2)}) async-start(bf16[2,256,6,256]{3,1,2,0:T(8,128)(2,1)} %get-tuple-element.4), calls=%async_computation.4 | async-start | bytes 3145728 | tf_op jit(solution)/shard_map/all_to_all | solution.py:55
  123.4 6.2 %collective-permute-start = (f32[2,1,128]{2,1,0:T(1,128)S(1)}, f32[2,1,128]{2,1,0:T(1,128)S(1)}, u32[]{:S(2)}, u32[]{:S(2)}) collective-permute-start(f32[2,1,128]{2,1,0:T(1,128)S(1)} %pad_maximum_fusion.2), channel_id=1, source_target_pairs={{0,254},{2,0},{4,2},{6,4},{8,6},{10,8},{12,10},{14,12},{16,14},{18... | collective-permute-start | bytes 3080 | tf_op jit(solution)/shard_map/ppermute | solution.py:68
  129.6 9.1 %pmax.28 = f32[]{:T(128)} all-reduce(f32[]{:T(128)} %get-tuple-element.2), channel_id=1, replica_groups=mesh['macro_0'=4,'macro_1'=2,'macro_2'=8,'macro_3'=2,'micro'=2] {'macro_0'}, use_global_device_ids=true, to_apply=%region_6.0 | all-reduce | flops 1 | bytes 8 | tf_op jit(solution)/shard_map/pmax | solution.py:61
  138.6 5.5 %pmax.29 = f32[]{:T(128)} all-reduce(f32[]{:T(128)} %pmax.28), channel_id=1, replica_groups=mesh['macro_0'=4,'macro_1'=2,'macro_2'=8,'macro_3'=2,'micro'=2] {'macro_1'}, use_global_device_ids=true, to_apply=%region_7.0 | all-reduce | flops 1 | bytes 8 | tf_op jit(solution)/shard_map/pmax | solution.py:61
  144.2 19.0 %pmax.30 = f32[]{:T(128)} all-reduce(f32[]{:T(128)} %pmax.29), channel_id=1, replica_groups=mesh['macro_0'=4,'macro_1'=2,'macro_2'=8,'macro_3'=2,'micro'=2] {'macro_2'}, use_global_device_ids=true, to_apply=%region_8.0 | all-reduce | flops 1 | bytes 8 | tf_op jit(solution)/shard_map/pmax | solution.py:61
  163.9 3.1 %pmax.31 = f32[]{:T(128)} all-reduce(f32[]{:T(128)} %pmax.30), channel_id=1, replica_groups=mesh['macro_0'=4,'macro_1'=2,'macro_2'=8,'macro_3'=2,'micro'=2] {'macro_3'}, use_global_device_ids=true, to_apply=%region_9.0 | all-reduce | flops 1 | bytes 8 | tf_op jit(solution)/shard_map/pmax | solution.py:61
  172.0 6.4 %collective-permute-done.1 = f32[1,128]{1,0:T(1,128)S(1)} collective-permute-done((f32[1,128]{1,0:T(1,128)S(1)}, f32[1,128]{1,0:T(1,128)S(1)}, u32[]{:S(2)}, u32[]{:S(2)}) %collective-permute-start.1) | collective-permute-done | bytes 544 | tf_op jit(solution)/shard_map/ppermute | solution.py:68
  (44 shorter events, 23.4 us)
Async XLA Ops:
  0.6 104.1 %copy-start = (f32[128]{0:T(128)S(1)}, f32[128]{0:T(128)}, u32[]{:S(2)}) copy-start(f32[128]{0:T(128)} %param.13) | copy-start | bytes 1540
  24.9 39.0 %all-to-all-start = ((bf16[512,12,256]{2,0,1:T(8,128)(2,1)}), bf16[512,12,256]{2,0,1:T(8,128)(2,1)S(1)}, u32[]{:S(2)}, u32[]{:S(2)}) async-start(bf16[512,12,256]{2,0,1:T(8,128)(2,1)} %param.8), calls=%async_computation | async-start | bytes 6291456 | tf_op jit(solution)/shard_map/all_to_all | solution.py:78
  32.1 6.3 %copy-start.1 = (f32[512,128]{1,0:T(8,128)S(1)}, f32[512,128]{1,0:T(8,128)}, u32[]{:S(2)}) copy-start(f32[512,128]{1,0:T(8,128)} %param.7) | copy-start | bytes 786436
  73.3 3.8 %copy-start.4 = (f32[512,512]{1,0:T(8,128)S(1)}, f32[512,512]{1,0:T(8,128)}, u32[]{:S(2)}) copy-start(f32[512,512]{1,0:T(8,128)} %copy.30) | copy-start | bytes 3145732
  73.3 3.8 %copy-start.7 = (bf16[512,512,1]{1,0,2:T(8,128)(2,1)S(1)}, bf16[512,512,1]{1,0,2:T(8,128)(2,1)}, u32[]{:S(2)}) copy-start(bf16[512,512,1]{1,0,2:T(8,128)(2,1)} %reshape.38) | copy-start | bytes 1572868
  79.2 2.1 %copy-start.6 = (bf16[512,2,256]{0,2,1:T(8,128)(2,1)S(1)}, bf16[512,2,256]{0,2,1:T(8,128)(2,1)}, u32[]{:S(2)}) copy-start(bf16[512,2,256]{0,2,1:T(8,128)(2,1)} %copy.36) | copy-start | bytes 1572868
  81.3 2.1 %copy-start.5 = (f32[128,2,256]{0,2,1:T(8,128)S(1)}, f32[128,2,256]{0,2,1:T(8,128)}, u32[]{:S(2)}) copy-start(f32[128,2,256]{0,2,1:T(8,128)} %get-tuple-element.7) | copy-start | bytes 786436
  85.2 10.6 %all-to-all-start.3 = ((bf16[2,512,128]{2,1,0:T(8,128)(2,1)}), bf16[2,512,128]{2,1,0:T(8,128)(2,1)}, u32[]{:S(2)}, u32[]{:S(2)}) async-start(bf16[2,512,128]{2,1,0:T(8,128)(2,1)} %broadcast_in_dim.16), calls=%async_computation.3 | async-start | bytes 524288 | tf_op jit(solution)/shard_map/all_to_all | solution.py:20
  94.8 10.2 %copy-start.8 = (f32[512]{0:T(512)S(1)}, f32[512]{0:T(512)}, u32[]{:S(2)}) copy-start(f32[512]{0:T(512)} %param.9) | copy-start | bytes 6148
  95.8 20.0 %all-to-all-start.5 = ((bf16[2,256,6,256]{3,1,2,0:T(8,128)(2,1)}), bf16[2,256,6,256]{3,1,2,0:T(8,128)(2,1)S(1)}, u32[]{:S(2)}, u32[]{:S(2)}) async-start(bf16[2,256,6,256]{3,1,2,0:T(8,128)(2,1)} %get-tuple-element.5), calls=%async_computation.5 | async-start | bytes 3145728 | tf_op jit(solution)/shard_map/all_to_all | solution.py:55
  104.0 0.7 copy-start.2
  115.8 64.5 %all-to-all-start.4 = ((bf16[2,256,6,256]{3,1,2,0:T(8,128)(2,1)}), bf16[2,256,6,256]{3,1,2,0:T(8,128)(2,1)S(1)}, u32[]{:S(2)}, u32[]{:S(2)}) async-start(bf16[2,256,6,256]{3,1,2,0:T(8,128)(2,1)} %get-tuple-element.4), calls=%async_computation.4 | async-start | bytes 3145728 | tf_op jit(solution)/shard_map/all_to_all | solution.py:55
  123.4 45.9 %collective-permute-start = (f32[2,1,128]{2,1,0:T(1,128)S(1)}, f32[2,1,128]{2,1,0:T(1,128)S(1)}, u32[]{:S(2)}, u32[]{:S(2)}) collective-permute-start(f32[2,1,128]{2,1,0:T(1,128)S(1)} %pad_maximum_fusion.2), channel_id=1, source_target_pairs={{0,254},{2,0},{4,2},{6,4},{8,6},{10,8},{12,10},{14,12},{16,14},{18... | collective-permute-start | bytes 3080 | tf_op jit(solution)/shard_map/ppermute | solution.py:68
  170.5 0.7 copy-start.3
  171.2 7.2 %collective-permute-start.1 = (f32[1,128]{1,0:T(1,128)S(1)}, f32[1,128]{1,0:T(1,128)S(1)}, u32[]{:S(2)}, u32[]{:S(2)}) collective-permute-start(f32[1,128]{1,0:T(1,128)S(1)} %slice.33), channel_id=1, source_target_pairs={{0,2},{2,4},{4,6},{6,8},{8,10},{10,12},{12,14},{14,16},{16,18},{18... | collective-permute-start | bytes 1544 | tf_op jit(solution)/shard_map/ppermute | solution.py:68
where the time goes:
time: 183 us; the launch traced here: 182 us
  blocking collectives  58.8 us (32%)
  waiting for transfers between devices  35.4 us (19%)
  starting transfers between devices  35 us (19%)
  local copies, waits for them, and re-layouts  28.4 us (16%)
  matrix products  13.4 us (7%)
  other arithmetic  9.2 us (5%)
  between operations  2.04 us (1%)
    pmax x4, blocking collectives, by_axis(): array = lax.pmax(array, axis)  36.7 us
    all_to_all x2, blocking collectives, sent_to_all(): return lax.all_to_all(copies, axis, split_axis=0, concat_axis=0, tiled=True)  22.1 us
    all_to_all x1, waiting for transfers between devices, shards(): lax.all_to_all(micro_state, 'micro', split_axis=1, concat_axis=2, tiled=T...  18.7 us
    all_to_all x2, starting transfers between devices, cut_exchange(): lax.all_to_all(section, axis, split_axis=0, concat_axis=0, tiled=True)  14.1 us
    dot_general x4, matrix products, shards(): jnp.dot(micro_now.reshape(-1, width), coupling, preferred_element_type=jn...  10 us
    all_to_all x2, waiting for transfers between devices, cut_exchange(): lax.all_to_all(section, axis, split_axis=0, concat_axis=0, tiled=True)  9.21 us
    all_to_all x1, starting transfers between devices, sent_to_all(): return lax.all_to_all(copies, axis, split_axis=0, concat_axis=0, tiled=True)  7.32 us
    all_to_all x1, starting transfers between devices, shards(): lax.all_to_all(micro_state, 'micro', split_axis=1, concat_axis=2, tiled=T...  7.27 us
  transfers between devices with their start and end apart: 6, of which 4 were waited for; matrix products, arithmetic and copies ran while one was open for 13% of the time, Pallas kernels for 0%

commit v1 on v0

--- a/solution.py
+++ b/solution.py
@@ -75,7 +75,11 @@
     forcing = jnp.tanh(
         jnp.dot(macro_state, forcing_full, precision=highest, preferred_element_type=jnp.float32)
     )
-    micro_now = lax.all_to_all(micro_state, "micro", split_axis=1, concat_axis=2, tiled=True)
+    s_next = lax.axis_size("micro")
+    aux = jnp.split(micro_state, s_next, axis=1)
+    part_now = jnp.stack(aux, axis=0)
+    local_now = lax.all_to_all(part_now, "micro", 0, 0)
+    micro_now = jnp.concatenate(local_now, axis=2)
     tanh_sum = jnp.zeros(forcing.shape, jnp.float32)
     width = micro_now.shape[2]
     for _ in range(STEPS):

time: 183 us -> 177 us (0.967)
  blocking collectives: 58.8 us -> 47.9 us
  starting transfers between devices: 35 us -> 41.5 us
  local copies, waits for them, and re-layouts: 28.4 us -> 23.9 us
  other arithmetic: 9.2 us -> 11.1 us
    all_to_all x2 -> x1, blocking collectives: 22.1 us -> 10.9 us  [sent_to_all(): return lax.all_to_all(copies, axis, split_axis=0, concat_axis=0, tiled=True)]
    all_to_all x1 -> x2, starting transfers between devices: 7.32 us -> 14.1 us  [sent_to_all(): return lax.all_to_all(copies, axis, split_axis=0, concat_axis=0, tiled=True)]
    all_to_all x1 -> x0, local copies, waits for them, and re-layouts: 4.9 us -> none  [shards(): lax.all_to_all(micro_state, 'micro', split_axis=1, concat_axis=2, tiled=T...]
    dot_general x1, local copies, waits for them, and re-layouts: 4.57 us -> 0.27 us  [shards(): jnp.dot(micro_now.reshape(-1, width), coupling, preferred_element_type=jn...]
    another operation x0 -> x1, local copies, waits for them, and re-layouts: none -> 2.08 us  [shards(): part_now = jnp.stack(aux, axis=0)]
    another operation x0 -> x1, other arithmetic: none -> 1.94 us  [shards(): part_now = jnp.stack(aux, axis=0)]
    unnamed x18 -> x20, local copies, waits for them, and re-layouts: 1.43 us -> 3.29 us
  transfers between devices with their start and end apart: 6 -> 7, of which waited for: 4 -> 5; matrix products, arithmetic and copies ran while one was open for 13% -> 16% of each run, Pallas kernels for 0% -> 0%
where the time goes in v1:
time: 177 us; the launch traced here: 176 us
  blocking collectives  47.9 us (27%)
  starting transfers between devices  41.5 us (23%)
  waiting for transfers between devices  36.3 us (21%)
  local copies, waits for them, and re-layouts  23.9 us (14%)
  matrix products  12.9 us (7%)
  other arithmetic  11.1 us (6%)
  between operations  2.1 us (1%)
    pmax x4, blocking collectives, by_axis(): array = lax.pmax(array, axis)  37 us
    all_to_all x1, waiting for transfers between devices, shards(): local_now = lax.all_to_all(part_now, 'micro', 0, 0)  18.7 us
    all_to_all x2, starting transfers between devices, sent_to_all(): return lax.all_to_all(copies, axis, split_axis=0, concat_axis=0, tiled=True)  14.1 us
    all_to_all x2, starting transfers between devices, cut_exchange(): lax.all_to_all(section, axis, split_axis=0, concat_axis=0, tiled=True)  13.9 us
    all_to_all x1, blocking collectives, sent_to_all(): return lax.all_to_all(copies, axis, split_axis=0, concat_axis=0, tiled=True)  10.9 us
    all_to_all x2, waiting for transfers between devices, cut_exchange(): lax.all_to_all(section, axis, split_axis=0, concat_axis=0, tiled=True)  9.47 us
    dot_general x4, matrix products, shards(): jnp.dot(micro_now.reshape(-1, width), coupling, preferred_element_type=jn...  9.44 us
    all_to_all x1, starting transfers between devices, shards(): local_now = lax.all_to_all(part_now, 'micro', 0, 0)  7.27 us
  transfers between devices with their start and end apart: 7, of which 5 were waited for; matrix products, arithmetic and copies ran while one was open for 16% of the time, Pallas kernels for 0%

profile of v1, /device:TPU:4, one launch (start us, length us, event | category | flops | bytes accessed | tf_op | source)
XLA Modules:
  0.0 175.6 jit_solution(17267120227450437310)
XLA Ops:
  1.8 10.9 %all_to_all.30 = f32[2,256,256]{1,2,0:T(8,128)} all-to-all(f32[2,256,256]{1,2,0:T(8,128)S(1)} %broadcast_in_dim.7), channel_id=1, replica_groups=mesh['macro_0'=4,'macro_1'=2,'macro_2'=8,'macro_3'=2,'micro'=2] {'micro'}, dimensions={0} | all-to-all | bytes 1048576 | tf_op jit(solution)/shard_map/all_to_all | solution.py:20
  14.5 6.7 %all-to-all-start.1 = ((bf16[2,512,256]{2,1,0:T(8,128)(2,1)}), bf16[2,512,256]{2,1,0:T(8,128)(2,1)S(1)}, u32[]{:S(2)}, u32[]{:S(2)}) async-start(bf16[2,512,256]{2,1,0:T(8,128)(2,1)} %broadcast_in_dim.6), calls=%async_computation.1 | async-start | bytes 1048576 | tf_op jit(solution)/shard_map/all_to_all | solution.py:20
  21.3 2.1 %slice_bitcast_fusion.1 = (bf16[1,512,6,256]{3,1,2,0:T(8,128)(2,1)S(1)}, bf16[1,512,6,256]{3,1,2,0:T(8,128)(2,1)S(1)}) fusion(bf16[512,12,256]{2,0,1:T(8,128)(2,1)} %param.8), kind=kLoop, calls=%fused_computation.12 | loop fusion | bytes 6291456 | tf_op jit(solution)/shard_map/stack | solution.py:80
  26.8 7.3 %all-to-all-start = ((bf16[2,512,6,256]{3,1,2,0:T(8,128)(2,1)}), bf16[2,512,6,256]{3,1,2,0:T(8,128)(2,1)S(1)}, u32[]{:S(2)}, u32[]{:S(2)}) async-start(bf16[2,512,6,256]{3,1,2,0:T(8,128)(2,1)} %pad_maximum_fusion), calls=%async_computation | async-start | bytes 6291456 | tf_op jit(solution)/shard_map/all_to_all | solution.py:81
  34.1 2.4 %copy.28 = bf16[512,2,256]{2,1,0:T(2,128)(2,1)} copy(bf16[512,2,256]{2,0,1:T(8,128)(2,1)} %bitcast.53) | data formatting | bytes 1048576 | tf_op jit(solution)/shard_map/transpose | solution.py:13
  36.5 2.0 %copy.36 = bf16[512,2,256]{0,2,1:T(8,128)(2,1)} copy(bf16[512,2,256]{2,0,1:T(8,128)(2,1)} %bitcast.54) | data formatting | bytes 1048576 | tf_op jit(solution)/shard_map/reshape | solution.py:15
  40.3 2.0 %fusion = f32[512,512]{0,1:T(8,128)} fusion(f32[128,512]{0,1:T(8,128)S(1)} %bitcast.61, f32[512,128]{1,0:T(8,128)S(1)} %copy-done.1), kind=kOutput, calls=%fused_computation.14 | convolution fusion | flops 402653184 | bytes 1572864 | tf_op jit(solution)/shard_map/dot_general | solution.py:76
  42.3 2.5 %copy.30 = f32[512,512]{1,0:T(8,128)} copy(f32[512,512]{0,1:T(8,128)} %fusion) | data formatting | bytes 2097152 | tf_op jit(solution)/shard_map/tanh | solution.py:75
  44.9 2.2 %reshape.40 = bf16[512,512,1]{1,0,2:T(8,128)(2,1)} reshape(bf16[512,2,256]{2,1,0:T(2,128)(2,1)} %copy.28) | data formatting | bytes 1048576 | tf_op jit(solution)/shard_map/reshape | solution.py:15
  47.0 18.7 %all-to-all-done = bf16[2,512,6,256]{3,1,2,0:T(8,128)(2,1)S(1)} async-done(((bf16[2,512,6,256]{3,1,2,0:T(8,128)(2,1)}), bf16[2,512,6,256]{3,1,2,0:T(8,128)(2,1)S(1)}, u32[]{:S(2)}, u32[]{:S(2)}) %all-to-all-start) | async-done | bytes 3145760 | tf_op jit(solution)/shard_map/all_to_all | solution.py:81
  67.1 2.3 %tanh_reduce_fusion.3 = (f32[512,512]{1,0:T(8,128)S(1)}, bf16[512,6,512]{2,0,1:T(8,128)(2,1)S(1)}) fusion(f32[512,512]{1,0:T(8,128)S(1)} %copy-done.5, bf16[512,6,512]{2,0,1:T(8,128)(2,1)S(1)} %bitcast.57, bf16[512,512,1]{1,0,2:T(8,128)(2,1)S(1)} %copy-done.8), kind=kOutput, calls=%fused_computation.6 | convolution fusion | flops 1616642048 | bytes 8912896 | tf_op jit(solution)/shard_map/dot_general | solution.py:86
  69.5 2.4 %tanh_reduce_fusion.2 = (f32[512,512]{1,0:T(8,128)S(1)}, bf16[512,6,512]{2,0,1:T(8,128)(2,1)S(1)}) fusion(f32[512,512]{1,0:T(8,128)S(1)} %copy-done.5, bf16[512,6,512]{2,0,1:T(8,128)(2,1)S(1)} %get-tuple-element.19, bf16[512,512,1]{1,0,2:T(8,128)(2,1)S(1)} %copy-done.8), kind=kOutput, calls=%fused_computation.4 | convolution fusion | flops 1616642048 | bytes 8912896 | tf_op jit(solution)/shard_map/dot_general | solution.py:86
  71.9 2.3 %tanh_reduce_fusion.1 = (f32[512,512]{1,0:T(8,128)S(1)}, bf16[512,6,512]{2,0,1:T(8,128)(2,1)S(1)}) fusion(f32[512,512]{1,0:T(8,128)S(1)} %copy-done.5, bf16[512,6,512]{2,0,1:T(8,128)(2,1)S(1)} %get-tuple-element.21, bf16[512,512,1]{1,0,2:T(8,128)(2,1)S(1)} %copy-done.8), kind=kOutput, calls=%fused_computation.2 | convolution fusion | flops 1616642048 | bytes 8912896 | tf_op jit(solution)/shard_map/dot_general | solution.py:86
  74.2 2.4 %tanh_reduce_fusion = (f32[512,512]{1,0:T(8,128)S(1)}, bf16[512,6,512]{2,0,1:T(8,128)(2,1)S(1)}) fusion(f32[512,512]{1,0:T(8,128)S(1)} %copy-done.5, bf16[512,6,512]{2,0,1:T(8,128)(2,1)S(1)} %get-tuple-element.17, bf16[512,512,1]{0,1,2:T(8,128)(2,1)S(1)} %bitcast.62), kind=kOutput, calls=%fused_computation | convolution fusion | flops 1616642048 | bytes 8912896 | tf_op jit(solution)/shard_map/dot_general | solution.py:86
  78.5 7.3 %all-to-all-start.3 = ((bf16[2,512,128]{2,1,0:T(8,128)(2,1)}), bf16[2,512,128]{2,1,0:T(8,128)(2,1)}, u32[]{:S(2)}, u32[]{:S(2)}) async-start(bf16[2,512,128]{2,1,0:T(8,128)(2,1)} %broadcast_in_dim.16), calls=%async_computation.3 | async-start | bytes 524288 | tf_op jit(solution)/shard_map/all_to_all | solution.py:20
  89.1 7.2 %all-to-all-start.5 = ((bf16[2,256,6,256]{3,1,2,0:T(8,128)(2,1)}), bf16[2,256,6,256]{3,1,2,0:T(8,128)(2,1)S(1)}, u32[]{:S(2)}, u32[]{:S(2)}) async-start(bf16[2,256,6,256]{3,1,2,0:T(8,128)(2,1)} %get-tuple-element.5), calls=%async_computation.5 | async-start | bytes 3145728 | tf_op jit(solution)/shard_map/all_to_all | solution.py:55
  99.8 9.5 %all-to-all-done.5 = bf16[2,256,6,256]{3,1,2,0:T(8,128)(2,1)S(1)} async-done(((bf16[2,256,6,256]{3,1,2,0:T(8,128)(2,1)}), bf16[2,256,6,256]{3,1,2,0:T(8,128)(2,1)S(1)}, u32[]{:S(2)}, u32[]{:S(2)}) %all-to-all-start.5) | async-done | bytes 1572896 | tf_op jit(solution)/shard_map/all_to_all | solution.py:55
  109.3 6.7 %all-to-all-start.4 = ((bf16[2,256,6,256]{3,1,2,0:T(8,128)(2,1)}), bf16[2,256,6,256]{3,1,2,0:T(8,128)(2,1)S(1)}, u32[]{:S(2)}, u32[]{:S(2)}) async-start(bf16[2,256,6,256]{3,1,2,0:T(8,128)(2,1)} %get-tuple-element.4), calls=%async_computation.4 | async-start | bytes 3145728 | tf_op jit(solution)/shard_map/all_to_all | solution.py:55
  116.7 6.1 %collective-permute-start = (f32[2,1,128]{2,1,0:T(1,128)S(1)}, f32[2,1,128]{2,1,0:T(1,128)S(1)}, u32[]{:S(2)}, u32[]{:S(2)}) collective-permute-start(f32[2,1,128]{2,1,0:T(1,128)S(1)} %pad_maximum_fusion.3), channel_id=1, source_target_pairs={{0,254},{2,0},{4,2},{6,4},{8,6},{10,8},{12,10},{14,12},{16,14},{18... | collective-permute-start | bytes 3080 | tf_op jit(solution)/shard_map/ppermute | solution.py:68
  122.8 9.1 %pmax.28 = f32[]{:T(128)} all-reduce(f32[]{:T(128)} %get-tuple-element.2), channel_id=1, replica_groups=mesh['macro_0'=4,'macro_1'=2,'macro_2'=8,'macro_3'=2,'micro'=2] {'macro_0'}, use_global_device_ids=true, to_apply=%region_6.0 | all-reduce | flops 1 | bytes 8 | tf_op jit(solution)/shard_map/pmax | solution.py:61
  131.9 5.6 %pmax.29 = f32[]{:T(128)} all-reduce(f32[]{:T(128)} %pmax.28), channel_id=1, replica_groups=mesh['macro_0'=4,'macro_1'=2,'macro_2'=8,'macro_3'=2,'micro'=2] {'macro_1'}, use_global_device_ids=true, to_apply=%region_7.0 | all-reduce | flops 1 | bytes 8 | tf_op jit(solution)/shard_map/pmax | solution.py:61
  137.5 19.1 %pmax.30 = f32[]{:T(128)} all-reduce(f32[]{:T(128)} %pmax.29), channel_id=1, replica_groups=mesh['macro_0'=4,'macro_1'=2,'macro_2'=8,'macro_3'=2,'micro'=2] {'macro_2'}, use_global_device_ids=true, to_apply=%region_8.0 | all-reduce | flops 1 | bytes 8 | tf_op jit(solution)/shard_map/pmax | solution.py:61
  157.3 3.1 %pmax.31 = f32[]{:T(128)} all-reduce(f32[]{:T(128)} %pmax.30), channel_id=1, replica_groups=mesh['macro_0'=4,'macro_1'=2,'macro_2'=8,'macro_3'=2,'micro'=2] {'macro_3'}, use_global_device_ids=true, to_apply=%region_9.0 | all-reduce | flops 1 | bytes 8 | tf_op jit(solution)/shard_map/pmax | solution.py:61
  165.5 6.4 %collective-permute-done.1 = f32[1,128]{1,0:T(1,128)S(1)} collective-permute-done((f32[1,128]{1,0:T(1,128)S(1)}, f32[1,128]{1,0:T(1,128)S(1)}, u32[]{:S(2)}, u32[]{:S(2)}) %collective-permute-start.1) | collective-permute-done | bytes 544 | tf_op jit(solution)/shard_map/ppermute | solution.py:68
  (48 shorter events, 27.0 us)
Async XLA Ops:
  0.6 97.3 %copy-start = (f32[128]{0:T(128)S(1)}, f32[128]{0:T(128)}, u32[]{:S(2)}) copy-start(f32[128]{0:T(128)} %param.13) | copy-start | bytes 1540
  14.5 11.5 %all-to-all-start.1 = ((bf16[2,512,256]{2,1,0:T(8,128)(2,1)}), bf16[2,512,256]{2,1,0:T(8,128)(2,1)S(1)}, u32[]{:S(2)}, u32[]{:S(2)}) async-start(bf16[2,512,256]{2,1,0:T(8,128)(2,1)} %broadcast_in_dim.6), calls=%async_computation.1 | async-start | bytes 1048576 | tf_op jit(solution)/shard_map/all_to_all | solution.py:20
  26.0 0.8 copy-start.2
  26.8 39.0 %all-to-all-start = ((bf16[2,512,6,256]{3,1,2,0:T(8,128)(2,1)}), bf16[2,512,6,256]{3,1,2,0:T(8,128)(2,1)S(1)}, u32[]{:S(2)}, u32[]{:S(2)}) async-start(bf16[2,512,6,256]{3,1,2,0:T(8,128)(2,1)} %pad_maximum_fusion), calls=%async_computation | async-start | bytes 6291456 | tf_op jit(solution)/shard_map/all_to_all | solution.py:81
  34.1 6.2 %copy-start.1 = (f32[512,128]{1,0:T(8,128)S(1)}, f32[512,128]{1,0:T(8,128)}, u32[]{:S(2)}) copy-start(f32[512,128]{1,0:T(8,128)} %param.7) | copy-start | bytes 786436
  65.8 1.2 copy-start.5
  65.8 1.4 copy-start.8
  71.8 2.4 %copy-start.7 = (bf16[512,2,256]{0,2,1:T(8,128)(2,1)S(1)}, bf16[512,2,256]{0,2,1:T(8,128)(2,1)}, u32[]{:S(2)}) copy-start(bf16[512,2,256]{0,2,1:T(8,128)(2,1)} %copy.36) | copy-start | bytes 1572868
  74.2 2.4 %copy-start.6 = (f32[128,2,256]{0,2,1:T(8,128)S(1)}, f32[128,2,256]{0,2,1:T(8,128)}, u32[]{:S(2)}) copy-start(f32[128,2,256]{0,2,1:T(8,128)} %get-tuple-element.9) | copy-start | bytes 786436
  78.5 10.6 %all-to-all-start.3 = ((bf16[2,512,128]{2,1,0:T(8,128)(2,1)}), bf16[2,512,128]{2,1,0:T(8,128)(2,1)}, u32[]{:S(2)}, u32[]{:S(2)}) async-start(bf16[2,512,128]{2,1,0:T(8,128)(2,1)} %broadcast_in_dim.16), calls=%async_computation.3 | async-start | bytes 524288 | tf_op jit(solution)/shard_map/all_to_all | solution.py:20
  88.1 10.2 %copy-start.9 = (f32[512]{0:T(512)S(1)}, f32[512]{0:T(512)}, u32[]{:S(2)}) copy-start(f32[512]{0:T(512)} %param.9) | copy-start | bytes 6148
  89.1 20.2 %all-to-all-start.5 = ((bf16[2,256,6,256]{3,1,2,0:T(8,128)(2,1)}), bf16[2,256,6,256]{3,1,2,0:T(8,128)(2,1)S(1)}, u32[]{:S(2)}, u32[]{:S(2)}) async-start(bf16[2,256,6,256]{3,1,2,0:T(8,128)(2,1)} %get-tuple-element.5), calls=%async_computation.5 | async-start | bytes 3145728 | tf_op jit(solution)/shard_map/all_to_all | solution.py:55
  97.3 0.7 copy-start.3
  109.3 64.5 %all-to-all-start.4 = ((bf16[2,256,6,256]{3,1,2,0:T(8,128)(2,1)}), bf16[2,256,6,256]{3,1,2,0:T(8,128)(2,1)S(1)}, u32[]{:S(2)}, u32[]{:S(2)}) async-start(bf16[2,256,6,256]{3,1,2,0:T(8,128)(2,1)} %get-tuple-element.4), calls=%async_computation.4 | async-start | bytes 3145728 | tf_op jit(solution)/shard_map/all_to_all | solution.py:55
  116.7 46.1 %collective-permute-start = (f32[2,1,128]{2,1,0:T(1,128)S(1)}, f32[2,1,128]{2,1,0:T(1,128)S(1)}, u32[]{:S(2)}, u32[]{:S(2)}) collective-permute-start(f32[2,1,128]{2,1,0:T(1,128)S(1)} %pad_maximum_fusion.3), channel_id=1, source_target_pairs={{0,254},{2,0},{4,2},{6,4},{8,6},{10,8},{12,10},{14,12},{16,14},{18... | collective-permute-start | bytes 3080 | tf_op jit(solution)/shard_map/ppermute | solution.py:68
  163.9 0.7 copy-start.4
  164.7 7.2 %collective-permute-start.1 = (f32[1,128]{1,0:T(1,128)S(1)}, f32[1,128]{1,0:T(1,128)S(1)}, u32[]{:S(2)}, u32[]{:S(2)}) collective-permute-start(f32[1,128]{1,0:T(1,128)S(1)} %slice.33), channel_id=1, source_target_pairs={{0,2},{2,4},{4,6},{6,8},{8,10},{10,12},{12,14},{14,16},{16,18},{18... | collective-permute-start | bytes 1544 | tf_op jit(solution)/shard_map/ppermute | solution.py:68
